TPU v7x, 32 devices: a whole 2x2x4 slice. The times are simulated.
32 devices in a mesh: temp: 8 (over y, x, core), bond: 4 (over z).
Axes of the slice: x: 2, y: 2, z: 4, core: 2. Of those that a mesh axis runs over, the one named last changes fastest.
Arguments:
- tensor: float32 [512, 4096], P(('temp', 'bond')), parts along dimension 0, may hold values from -6 to 6
- isometries: float32 [24, 64, 4096], P('temp', 'bond'), parts along dimension 0, may hold values from -0.09375 to 0.09375
Outputs:
- final_tensor: float32 [512, 4096], P(('temp', 'bond')), parts along dimension 0
- log_density: float32 [8], P('temp'), parts along dimension 0
There are 8 independent parts, one for each index of `temp`. A program takes and returns all parts, laid end to end along the dimension named above; each array names one. Nothing has to cross between parts.
All inputs are finite; a program needn't handle non-finite values. Where the computation divides by a largest or mean magnitude, that divisor is 1e-20 or more.
Results may differ from a plain program's by a relative error of at most 0.00027.
Values sent between devices are 32-bit elements; how exact they have to be, the bound alone decides.
No kernel may reach another device: no remote copies, remote signals or barrier semaphores. Data moves between devices by JAX's collectives and lax.ppermute only.
A program may use at most 128 MiB of HBM per device.

v0:
```python
import functools

import jax
import jax.numpy as jnp
from jax import lax
from jax.experimental import pallas as pl
from jax.experimental.pallas import tpu as pltpu
from jax.sharding import PartitionSpec as P


EPSILON = 1e-06
LANES = 128
PITCH = 72
BF16 = jnp.bfloat16
F32 = jnp.float32


def split_isometry(rows, width, u_ref, spread):
    low_half = lax.broadcasted_iota(jnp.int32, (rows, LANES), 1) < width
    for x in range(width // 2):
        value = u_ref[:, x * LANES : (x + 1) * LANES]
        high = value.astype(BF16).astype(F32)
        low = value - high
        turned = pltpu.roll(high, width, 1)
        for at, highs, lows in (
            (2 * x, jnp.where(low_half, high, turned), low),
            (2 * x + 1, jnp.where(low_half, turned, high), pltpu.roll(low, width, 1)),
        ):
            spread[pl.ds(at, rows, stride=PITCH), :] = highs
            spread[pl.ds(rows * PITCH + at, rows, stride=PITCH), :] = lows


def contract(rows, width, wired, stacked, factor, u_ref, out_ref, placed, spread):
    split_isometry(rows, width, u_ref, spread)
    pairs = width // 2
    groups = pairs // 4
    cells = width * width
    low_half = lax.broadcasted_iota(jnp.int32, (pairs, LANES), 1) < width

    def first(q, g):
        blocks = []
        for n in range(4):
            at = pl.multiple_of((4 * q + n) * PITCH, 8)
            highs = spread[pl.ds(at, width), :]
            lows = spread[pl.ds(rows * PITCH + at, width), :]
            blocks.append(jnp.concatenate([highs, lows[:, :width]], axis=1))
        u = jnp.concatenate(blocks, axis=0).astype(BF16)
        return jnp.dot(u, stacked[:, g * 512 : (g + 1) * 512], preferred_element_type=F32)

    def second(inner, g):
        high = inner.astype(BF16)
        low = (inner - high.astype(F32)).astype(BF16)

        def block(array, i):
            return jnp.concatenate(
                [array[n * width : (n + 1) * width, i * LANES : (i + 1) * LANES] for n in range(4)],
                axis=1,
            )

        highs = [block(high, i) for i in range(4)]
        lows = [block(low, i) for i in range(4)]
        weights = jnp.concatenate([h for h in highs for _ in range(2)] + lows, axis=0)
        return jnp.dot(
            factor[:, g * 768 : (g + 1) * 768], weights, preferred_element_type=F32
        )

    def finish_quad(q, total, peak):
        for n in range(4):
            part = total[:, n * LANES : (n + 1) * LANES]
            even0, odd0, even1, odd1 = (part[r * pairs : (r + 1) * pairs] for r in range(4))
            kept = jnp.where(low_half, even0, odd1)
            moved = jnp.where(low_half, odd0, even1)
            value = kept + pltpu.roll(moved, width, 1)
            peak = jnp.maximum(peak, jnp.abs(value))
            at = (q // 2) * (8 * pairs) + (q % 2) * 4 + n
            placed[pl.ds(at, pairs, stride=8), :] = value
        return peak

    def several(count, start, peak):
        steps = [(start + r, g) for r in range(count) for g in range(groups)]
        total = None
        inner = first(*steps[0])
        for k, (q, g) in enumerate(steps):
            ahead = first(*steps[k + 1]) if k + 1 < len(steps) else None
            update = second(inner, g)
            total = update if g == 0 else total + update
            if g + 1 == groups:
                peak = finish_quad(q, total, peak)
            inner = ahead
        return peak

    peak = jnp.zeros((pairs, LANES), F32)
    quads = rows // 4
    each = 2 if quads % 2 == 0 else 1
    peak = lax.fori_loop(0, quads // each, lambda i, p: several(each, i * each, p), peak)
    highest = jnp.max(peak)
    tall = min(rows, 8)
    for h in range(rows // tall):
        for x in range(pairs):
            at = (h * pairs + x) * 8
            out_ref[h * tall : (h + 1) * tall, x * LANES : (x + 1) * LANES] = placed[at : at + tall, :]
    if wired:
        out_ref[:, cells:] = jnp.full((rows, LANES), highest, F32)
    return highest


def level_kernel(count, scaled, section, wired, rows, width, sources, *refs):
    pieces = refs[:count]
    u_ref, before_ref, out_ref, notes_ref, stacked, factor = refs[count : count + 6]
    whole, turned, placed, spread = refs[count + 6 :]
    held = pieces[0].shape[0]
    pairs = width // 2
    cells = width * width
    found = sources(lax.axis_index("bond"))
    log_density = before_ref[4:8, :]
    inverse = None
    if scaled:
        largest = jnp.max(pieces[0][:, cells:])
        for piece in pieces[1:]:
            largest = jnp.maximum(largest, jnp.max(piece[:, cells:]))
        largest = jnp.full((4, LANES), largest, F32) + EPSILON
        log_density = log_density + jnp.log(largest) * 0.5**section
        inverse = (1.0 / largest)[0:1, :]
    for j in range(count):
        start = pl.multiple_of(found[j] * held, 8)
        for x in range(pairs):
            value = pieces[j][:, x * LANES : (x + 1) * LANES]
            if scaled:
                value = value * inverse
            whole[pl.ds(start, held), x * LANES : (x + 1) * LANES] = value

    for x in range(pairs):
        lanes = slice(x * LANES, (x + 1) * LANES)
        value = whole[:, lanes]
        high = value.astype(BF16)
        high_wide = high.astype(F32)
        low = (value - high_wide).astype(BF16)
        stacked[0:width, lanes] = high
        stacked[width : 2 * width, lanes] = low
        stacked[2 * width : 3 * width, lanes] = high
        both = jnp.concatenate([high_wide, low.astype(F32)], axis=0).T
        turned[pl.ds(x, width, stride=PITCH), :] = both[:width]
        turned[pl.ds(pairs + x, width, stride=PITCH), :] = both[width:]

    groups = pairs // 4
    for g in range(groups):
        blocks = []
        for i in range(4):
            b = 2 * (4 * g + i)
            upper = turned[b * PITCH : b * PITCH + width, :].astype(BF16)
            lower = turned[(b + 1) * PITCH : (b + 1) * PITCH + width, :].astype(BF16)
            blocks.append(jnp.concatenate([upper, lower], axis=0))
        highs = [
            jnp.concatenate([blocks[i][:, :width], blocks[i + 1][:, :width]], axis=1)
            for i in (0, 2)
        ]
        factor[:, g * 768 : (g + 1) * 768] = jnp.concatenate(blocks + highs, axis=1)

    highest = contract(rows, width, wired, stacked, factor, u_ref, out_ref, placed, spread)
    notes_ref[0:4, :] = jnp.full((4, LANES), highest, F32)
    notes_ref[4:8, :] = log_density


def more_kernel(wired, rows, width, stacked, factor, u_ref, before_ref, out_ref, notes_ref, placed, spread):
    highest = contract(rows, width, wired, stacked, factor, u_ref, out_ref, placed, spread)
    notes_ref[0:4, :] = jnp.maximum(before_ref[0:4, :], highest)
    notes_ref[4:8, :] = before_ref[4:8, :]


def cost(rows, width):
    products = 2 * rows * width**4
    return pl.CostEstimate(flops=6 * products, bytes_accessed=16 * width**3, transcendentals=0)


def params():
    return pltpu.CompilerParams(vmem_limit_bytes=32 * 1024 * 1024)


def level(pieces, sources, isometry, notes, section, wired):
    width = sum(piece.shape[0] for piece in pieces)
    rows, cells = isometry.shape
    span = cells + LANES if wired else cells
    return pl.pallas_call(
        functools.partial(
            level_kernel, len(pieces), section > 0, section, wired, rows, width, sources
        ),
        out_shape=[
            jax.ShapeDtypeStruct((rows, span), F32),
            jax.ShapeDtypeStruct((8, LANES), F32),
            jax.ShapeDtypeStruct((3 * width, cells), BF16),
            jax.ShapeDtypeStruct((2 * width, 96 * width), BF16),
        ],
        scratch_shapes=[
            pltpu.VMEM((width, cells), F32),
            pltpu.VMEM((width * PITCH, LANES), F32),
            pltpu.VMEM((max(rows, 8) * width // 2, LANES), F32),
            pltpu.VMEM((2 * rows * PITCH, LANES), F32),
        ],
        compiler_params=params(),
        cost_estimate=cost(rows, width),
        name="level",
    )(*pieces, isometry, notes)


def more(stacked, factor, isometry, notes, wired):
    width = stacked.shape[0] // 3
    rows, cells = isometry.shape
    span = cells + LANES if wired else cells
    return pl.pallas_call(
        functools.partial(more_kernel, wired, rows, width),
        out_shape=[
            jax.ShapeDtypeStruct((rows, span), F32),
            jax.ShapeDtypeStruct((8, LANES), F32),
        ],
        scratch_shapes=[
            pltpu.VMEM((max(rows, 8) * width // 2, LANES), F32),
            pltpu.VMEM((2 * rows * PITCH, LANES), F32),
        ],
        compiler_params=params(),
        cost_estimate=cost(rows, width),
        name="more",
    )(stacked, factor, isometry, notes)


def middle_sources(me):
    return [me, me ^ 1, me ^ 3, me ^ 2]


def on_line(tensor, isometries):
    sections = isometries.shape[0]
    send = lambda x, pairs: lax.ppermute(x, "bond", pairs)
    inward, swap, outward = [(0, 1), (3, 2)], [(1, 2), (2, 1)], [(1, 0), (2, 3)]
    far = send(tensor, [(0, 2), (3, 1)])
    near = send(tensor, inward)
    other = send(tensor, swap)
    pieces = [tensor, near, other, far]
    theirs = [send(isometries[0], inward)]
    later = send(isometries[1:], inward)
    theirs += [later[k] for k in range(sections - 1)]
    notes = jnp.zeros((8, LANES), F32)
    for section in range(sections):
        last = section + 1 == sections
        mine = isometries[section]
        order = [theirs[section], mine] if last else [mine, theirs[section]]
        first, notes, stacked, factor = level(
            pieces, middle_sources, order[0], notes, section, not last
        )
        if last:
            break
        first_other = send(first, swap)
        second, notes = more(stacked, factor, order[1], notes, True)
        second_other = send(second, swap)
        pieces = [first, second, first_other, second_other]
    moved = send(first, outward)
    second, notes = more(stacked, factor, order[1], notes, False)
    found = [notes, send(notes, swap), send(notes, outward), send(notes, [(1, 3), (2, 0)])]
    return pl.pallas_call(
        functools.partial(line_finish_kernel, sections),
        out_shape=[
            jax.ShapeDtypeStruct(tensor.shape, F32),
            jax.ShapeDtypeStruct((8, LANES), F32),
        ],
        compiler_params=params(),
        name="finish",
    )(second, moved, *found)


def line_finish_kernel(sections, second_ref, moved_ref, own, swapped, near, far, out_ref, log_ref):
    me = lax.axis_index("bond")
    inner = jnp.logical_or(me == 1, me == 2)

    def write(value_ref, one, two):
        largest = jnp.maximum(one[0:4, :], two[0:4, :]) + EPSILON
        log_density = one[4:8, :] + jnp.log(largest) * 0.5**sections
        log_ref[0:4, :] = log_density
        log_ref[4:8, :] = log_density
        out_ref[...] = value_ref[...] / largest[0:1, 0:1]

    @pl.when(inner)
    def _():
        write(second_ref, own, swapped)

    @pl.when(jnp.logical_not(inner))
    def _():
        write(moved_ref, near, far)


def gathered(tensor, isometries):
    sections = isometries.shape[0]
    own = tensor
    notes = jnp.zeros((8, LANES), F32)
    for section in range(sections):
        piece = lax.all_gather(own, "bond", axis=0, tiled=True)
        own, notes, _, _ = level(
            [piece],
            lambda me: [0],
            isometries[section],
            notes,
            section,
            section + 1 < sections,
        )
    largest = lax.pmax(notes[0, :1], "bond") + EPSILON
    return own / largest[0], notes[4, :1] + jnp.log(largest) * 0.5**sections


def on_device(tensor, isometries):
    if lax.axis_size("bond") == 4:
        final, log_density = on_line(tensor, isometries)
        return final, log_density[0, :1]
    return gathered(tensor, isometries)


def solution(mesh):
    in_specs = (P(("temp", "bond"), None), P("temp", "bond", None))
    out_specs = (P(("temp", "bond"), None), P("temp"))
    return jax.shard_map(
        on_device, mesh=mesh, in_specs=in_specs, out_specs=out_specs, check_vma=False
    )
```

profile of v0, /device:TPU:0, one launch (start us, length us, event | category | flops | bytes accessed | tf_op | source)
XLA Modules:
  0.0 101.6 jit_solution(13344710242049940891)
XLA Ops:
  0.6 5.1 %collective-permute-start = (f32[16,4096]{1,0:T(8,128)}, f32[16,4096]{1,0:T(8,128)S(1)}, u32[]{:S(2)}, u32[]{:S(2)}) collective-permute-start(f32[16,4096]{1,0:T(8,128)} %refs_0_.1), channel_id=1, source_target_pairs={{0,1},{3,2},{4,5},{7,6},{8,9},{11,10},{12,13},{15,14},{16,17},{19,... | collective-permute-start | bytes 786440 | tf_op jit(solution)/shard_map/ppermute | solution.py:231
  5.8 0.7 collective-permute-start.1
  6.4 4.0 %collective-permute-start.2 = (f32[16,4096]{1,0:T(8,128)}, f32[16,4096]{1,0:T(8,128)S(1)}, u32[]{:S(2)}, u32[]{:S(2)}) collective-permute-start(f32[16,4096]{1,0:T(8,128)} %refs_0_.1), channel_id=1, source_target_pairs={{0,2},{3,1},{4,6},{7,5},{8,10},{11,9},{12,14},{15,13},{16,18},{19,... | collective-permute-start | bytes 786440 | tf_op jit(solution)/shard_map/ppermute | solution.py:231
  10.4 1.2 %slice_bitcast_fusion.2 = (f32[16,4096]{1,0:T(8,128)S(1)}, f32[16,4096]{1,0:T(8,128)S(1)}, f32[16,4096]{1,0:T(8,128)S(1)}) fusion(f32[3,16,4096]{2,1,0:T(8,128)} %param.3), kind=kLoop, calls=%fused_computation.2 | loop fusion | bytes 1572864 | tf_op jit(solution)/shard_map/squeeze | solution.py:243
  11.6 1.4 %collective-permute-start.3 = (f32[16,4096]{1,0:T(8,128)S(1)}, f32[16,4096]{1,0:T(8,128)S(1)}, u32[]{:S(2)}, u32[]{:S(2)}) collective-permute-start(f32[16,4096]{1,0:T(8,128)S(1)} %get-tuple-element.44.refs_4_), channel_id=1, source_target_pairs={{0,1},{3,2},{4,5},{7,6},{8,9},{11,10},{12,13},{15,14},{16,17},{19,... | collective-permute-start | bytes 786440 | tf_op jit(solution)/shard_map/ppermute | solution.py:231
  13.1 1.3 %collective-permute-start.6 = (f32[2,16,4096]{2,1,0:T(8,128)S(1)}, f32[2,16,4096]{2,1,0:T(8,128)S(1)}, u32[]{:S(2)}, u32[]{:S(2)}) collective-permute-start(f32[2,16,4096]{2,1,0:T(8,128)S(1)} %slice.24), channel_id=1, source_target_pairs={{0,1},{3,2},{4,5},{7,6},{8,9},{11,10},{12,13},{15,14},{16,17},{19,... | collective-permute-start | bytes 1572872 | tf_op jit(solution)/shard_map/ppermute | solution.py:231
  14.4 0.0 collective-permute-done.refs_1_
  14.4 0.0 collective-permute-done.1.refs_2_
  14.4 4.0 %collective-permute-done.2.refs_3_ = f32[16,4096]{1,0:T(8,128)S(1)} collective-permute-done((f32[16,4096]{1,0:T(8,128)}, f32[16,4096]{1,0:T(8,128)S(1)}, u32[]{:S(2)}, u32[]{:S(2)}) %collective-permute-start.2) | collective-permute-done | bytes 262176 | tf_op jit(solution)/shard_map/ppermute | solution.py:231
  18.4 7.3 %level.3 = (f32[16,4224]{1,0:T(8,128)S(1)}, f32[8,128]{1,0:T(8,128)S(1)}, bf16[192,4096]{1,0:T(8,128)(2,1)S(1)}, bf16[128,6144]{1,0:T(8,128)(2,1)S(1)}) custom-call(f32[16,4096]{1,0:T(8,128)S(1)} %copy-done, f32[16,4096]{1,0:T(8,128)S(1)} %collective-permute-done.refs_1_, f32[16,4096]{1,0:T(8,128)S(1)} %collective-permute-done.1.refs_2_, ...), custom_call_target="tpu_custom_call" | custom-call | flops 3221225472 | bytes 4194304 | tf_op jit(solution)/shard_map/level/pallas_call | solution.py:183
  25.7 0.0 collective-permute-done.3.u_ref
  25.7 6.5 %more.3 = (f32[16,4224]{1,0:T(8,128)S(1)}, f32[8,128]{1,0:T(8,128)S(1)}) custom-call(bf16[192,4096]{1,0:T(8,128)(2,1)S(1)} %get-tuple-element.23.stacked, bf16[128,6144]{1,0:T(8,128)(2,1)S(1)} %get-tuple-element.24.factor, f32[16,4096]{1,0:T(8,128)S(1)} %collective-permute-done.3.u_ref, f32[8,128]{1,0:T(8,128)S(1)} %get-tuple-element.25.before_ref), custom_call_target="tpu_custom_call" | custom-call | flops 3221225472 | bytes 4194304 | tf_op jit(solution)/shard_map/more/pallas_call | solution.py:209
  32.3 0.7 collective-permute-start.5
  33.0 0.9 collective-permute-start.4
  33.8 0.2 collective-permute-done.6
  34.1 0.0 collective-permute-done.5.refs_3_
  34.1 7.5 %level.4 = (f32[16,4224]{1,0:T(8,128)S(1)}, f32[8,128]{1,0:T(8,128)S(1)}, bf16[192,4096]{1,0:T(8,128)(2,1)S(1)}, bf16[128,6144]{1,0:T(8,128)(2,1)S(1)}) custom-call(f32[16,4224]{1,0:T(8,128)S(1)} %get-tuple-element.22.refs_0_, f32[16,4224]{1,0:T(8,128)S(1)} %get-tuple-element.26.refs_1_, f32[16,4224]{1,0:T(8,128)S(1)} %collective-permute-done.4.refs_2_, ...), custom_call_target="tpu_custom_call" | custom-call | flops 3221225472 | bytes 4194304 | tf_op jit(solution)/shard_map/level/pallas_call | solution.py:183
  41.6 6.7 %more.4 = (f32[16,4224]{1,0:T(8,128)S(1)}, f32[8,128]{1,0:T(8,128)S(1)}) custom-call(bf16[192,4096]{1,0:T(8,128)(2,1)S(1)} %get-tuple-element.29.stacked, bf16[128,6144]{1,0:T(8,128)(2,1)S(1)} %get-tuple-element.30.factor, f32[16,4096]{1,0:T(8,128)S(1)} %get-tuple-element.46.u_ref, f32[8,128]{1,0:T(8,128)S(1)} %get-tuple-element.31.before_ref), custom_call_target="tpu_custom_call" | custom-call | flops 3221225472 | bytes 4194304 | tf_op jit(solution)/shard_map/more/pallas_call | solution.py:209
  48.3 0.7 collective-permute-start.8
  49.0 0.7 collective-permute-start.7
  49.7 0.0 collective-permute-done.8.refs_3_
  49.7 0.0 collective-permute-done.7.refs_2_
  49.7 7.6 %level.5 = (f32[16,4096]{1,0:T(8,128)S(1)}, f32[8,128]{1,0:T(8,128)S(1)}, bf16[192,4096]{1,0:T(8,128)(2,1)S(1)}, bf16[128,6144]{1,0:T(8,128)(2,1)S(1)}) custom-call(f32[16,4224]{1,0:T(8,128)S(1)} %get-tuple-element.28.refs_0_, f32[16,4224]{1,0:T(8,128)S(1)} %get-tuple-element.32.refs_1_, f32[16,4224]{1,0:T(8,128)S(1)} %collective-permute-done.7.refs_2_, ...), custom_call_target="tpu_custom_call" | custom-call | flops 3221225472 | bytes 4194304 | tf_op jit(solution)/shard_map/level/pallas_call | solution.py:183
  57.3 1.5 %collective-permute-start.9 = (f32[16,4096]{1,0:T(8,128)S(1)}, f32[16,4096]{1,0:T(8,128)S(1)}, u32[]{:S(2)}, u32[]{:S(2)}) collective-permute-start(f32[16,4096]{1,0:T(8,128)S(1)} %get-tuple-element.38), channel_id=1, source_target_pairs={{1,0},{2,3},{5,4},{6,7},{9,8},{10,11},{13,12},{14,15},{17,16},{18,... | collective-permute-start | bytes 786440 | tf_op jit(solution)/shard_map/ppermute | solution.py:231
  58.8 6.7 %more.5 = (f32[16,4096]{1,0:T(8,128)S(1)}, f32[8,128]{1,0:T(8,128)S(1)}) custom-call(bf16[192,4096]{1,0:T(8,128)(2,1)S(1)} %get-tuple-element.34.stacked, bf16[128,6144]{1,0:T(8,128)(2,1)S(1)} %get-tuple-element.35.factor, f32[16,4096]{1,0:T(8,128)S(1)} %get-tuple-element.42.u_ref, f32[8,128]{1,0:T(8,128)S(1)} %get-tuple-element.36.before_ref), custom_call_target="tpu_custom_call" | custom-call | flops 3221225472 | bytes 4194304 | tf_op jit(solution)/shard_map/more/pallas_call | solution.py:209
  65.6 0.7 collective-permute-start.10
  66.2 1.3 %collective-permute-start.11 = (f32[8,128]{1,0:T(8,128)S(1)}, f32[8,128]{1,0:T(8,128)S(1)}, u32[]{:S(2)}, u32[]{:S(2)}) collective-permute-start(f32[8,128]{1,0:T(8,128)S(1)} %get-tuple-element.39.own), channel_id=1, source_target_pairs={{1,0},{2,3},{5,4},{6,7},{9,8},{10,11},{13,12},{14,15},{17,16},{18,... | collective-permute-start | bytes 12296 | tf_op jit(solution)/shard_map/ppermute | solution.py:231
  67.5 1.3 %collective-permute-start.12 = (f32[8,128]{1,0:T(8,128)S(1)}, f32[8,128]{1,0:T(8,128)S(1)}, u32[]{:S(2)}, u32[]{:S(2)}) collective-permute-start(f32[8,128]{1,0:T(8,128)S(1)} %get-tuple-element.39.own), channel_id=1, source_target_pairs={{1,3},{2,0},{5,7},{6,4},{9,11},{10,8},{13,15},{14,12},{17,19},{18,... | collective-permute-start | bytes 12296 | tf_op jit(solution)/shard_map/ppermute | solution.py:231
  68.8 29.8 %collective-permute-done.11.near = f32[8,128]{1,0:T(8,128)S(1)} collective-permute-done((f32[8,128]{1,0:T(8,128)S(1)}, f32[8,128]{1,0:T(8,128)S(1)}, u32[]{:S(2)}, u32[]{:S(2)}) %collective-permute-start.11) | collective-permute-done | bytes 4128 | tf_op jit(solution)/shard_map/ppermute | solution.py:231
  98.7 1.6 %collective-permute-done.12.far = f32[8,128]{1,0:T(8,128)S(1)} collective-permute-done((f32[8,128]{1,0:T(8,128)S(1)}, f32[8,128]{1,0:T(8,128)S(1)}, u32[]{:S(2)}, u32[]{:S(2)}) %collective-permute-start.12) | collective-permute-done | bytes 4128 | tf_op jit(solution)/shard_map/ppermute | solution.py:231
  100.3 0.8 finish.1
  101.1 0.5 slice.28
  (10 shorter events, 0.1 us)
Async XLA Ops:
  0.6 17.8 %copy-start = (f32[16,4096]{1,0:T(8,128)S(1)}, f32[16,4096]{1,0:T(8,128)}, u32[]{:S(2)}) copy-start(f32[16,4096]{1,0:T(8,128)} %refs_0_.1) | copy-start | bytes 786436
  0.6 12.4 %copy-start.1 = (f32[3,16,4096]{2,1,0:T(8,128)S(1)}, f32[3,16,4096]{2,1,0:T(8,128)}, u32[]{:S(2)}) copy-start(f32[3,16,4096]{2,1,0:T(8,128)} %param.3) | copy-start | bytes 2359300
  0.6 13.8 %collective-permute-start = (f32[16,4096]{1,0:T(8,128)}, f32[16,4096]{1,0:T(8,128)S(1)}, u32[]{:S(2)}, u32[]{:S(2)}) collective-permute-start(f32[16,4096]{1,0:T(8,128)} %refs_0_.1), channel_id=1, source_target_pairs={{0,1},{3,2},{4,5},{7,6},{8,9},{11,10},{12,13},{15,14},{16,17},{19,... | collective-permute-start | bytes 786440 | tf_op jit(solution)/shard_map/ppermute | solution.py:231
  5.8 8.7 %collective-permute-start.1 = (f32[16,4096]{1,0:T(8,128)}, f32[16,4096]{1,0:T(8,128)S(1)}, u32[]{:S(2)}, u32[]{:S(2)}) collective-permute-start(f32[16,4096]{1,0:T(8,128)} %refs_0_.1), channel_id=1, source_target_pairs={{1,2},{2,1},{5,6},{6,5},{9,10},{10,9},{13,14},{14,13},{17,18},{18,... | collective-permute-start | bytes 786440 | tf_op jit(solution)/shard_map/ppermute | solution.py:231
  6.4 12.0 %collective-permute-start.2 = (f32[16,4096]{1,0:T(8,128)}, f32[16,4096]{1,0:T(8,128)S(1)}, u32[]{:S(2)}, u32[]{:S(2)}) collective-permute-start(f32[16,4096]{1,0:T(8,128)} %refs_0_.1), channel_id=1, source_target_pairs={{0,2},{3,1},{4,6},{7,5},{8,10},{11,9},{12,14},{15,13},{16,18},{19,... | collective-permute-start | bytes 786440 | tf_op jit(solution)/shard_map/ppermute | solution.py:231
  11.6 14.1 %collective-permute-start.3 = (f32[16,4096]{1,0:T(8,128)S(1)}, f32[16,4096]{1,0:T(8,128)S(1)}, u32[]{:S(2)}, u32[]{:S(2)}) collective-permute-start(f32[16,4096]{1,0:T(8,128)S(1)} %get-tuple-element.44.refs_4_), channel_id=1, source_target_pairs={{0,1},{3,2},{4,5},{7,6},{8,9},{11,10},{12,13},{15,14},{16,17},{19,... | collective-permute-start | bytes 786440 | tf_op jit(solution)/shard_map/ppermute | solution.py:231
  13.1 20.9 %collective-permute-start.6 = (f32[2,16,4096]{2,1,0:T(8,128)S(1)}, f32[2,16,4096]{2,1,0:T(8,128)S(1)}, u32[]{:S(2)}, u32[]{:S(2)}) collective-permute-start(f32[2,16,4096]{2,1,0:T(8,128)S(1)} %slice.24), channel_id=1, source_target_pairs={{0,1},{3,2},{4,5},{7,6},{8,9},{11,10},{12,13},{15,14},{16,17},{19,... | collective-permute-start | bytes 1572872 | tf_op jit(solution)/shard_map/ppermute | solution.py:231
  32.3 1.8 %collective-permute-start.5 = (f32[16,4224]{1,0:T(8,128)S(1)}, f32[16,4224]{1,0:T(8,128)S(1)}, u32[]{:S(2)}, u32[]{:S(2)}) collective-permute-start(f32[16,4224]{1,0:T(8,128)S(1)} %get-tuple-element.26.refs_1_), channel_id=1, source_target_pairs={{1,2},{2,1},{5,6},{6,5},{9,10},{10,9},{13,14},{14,13},{17,18},{18,... | collective-permute-start | bytes 811016 | tf_op jit(solution)/shard_map/ppermute | solution.py:231
  33.0 1.1 %collective-permute-start.4 = (f32[16,4224]{1,0:T(8,128)S(1)}, f32[16,4224]{1,0:T(8,128)S(1)}, u32[]{:S(2)}, u32[]{:S(2)}) collective-permute-start(f32[16,4224]{1,0:T(8,128)S(1)} %get-tuple-element.22.refs_0_), channel_id=1, source_target_pairs={{1,2},{2,1},{5,6},{6,5},{9,10},{10,9},{13,14},{14,13},{17,18},{18,... | collective-permute-start | bytes 811016 | tf_op jit(solution)/shard_map/ppermute | solution.py:231
  48.3 1.4 %collective-permute-start.8 = (f32[16,4224]{1,0:T(8,128)S(1)}, f32[16,4224]{1,0:T(8,128)S(1)}, u32[]{:S(2)}, u32[]{:S(2)}) collective-permute-start(f32[16,4224]{1,0:T(8,128)S(1)} %get-tuple-element.32.refs_1_), channel_id=1, source_target_pairs={{1,2},{2,1},{5,6},{6,5},{9,10},{10,9},{13,14},{14,13},{17,18},{18,... | collective-permute-start | bytes 811016 | tf_op jit(solution)/shard_map/ppermute | solution.py:231
  49.0 0.7 collective-permute-start.7
  57.3 43.0 %collective-permute-start.9 = (f32[16,4096]{1,0:T(8,128)S(1)}, f32[16,4096]{1,0:T(8,128)S(1)}, u32[]{:S(2)}, u32[]{:S(2)}) collective-permute-start(f32[16,4096]{1,0:T(8,128)S(1)} %get-tuple-element.38), channel_id=1, source_target_pairs={{1,0},{2,3},{5,4},{6,7},{9,8},{10,11},{13,12},{14,15},{17,16},{18,... | collective-permute-start | bytes 786440 | tf_op jit(solution)/shard_map/ppermute | solution.py:231
  65.6 3.3 %collective-permute-start.10 = (f32[8,128]{1,0:T(8,128)S(1)}, f32[8,128]{1,0:T(8,128)S(1)}, u32[]{:S(2)}, u32[]{:S(2)}) collective-permute-start(f32[8,128]{1,0:T(8,128)S(1)} %get-tuple-element.39.own), channel_id=1, source_target_pairs={{1,2},{2,1},{5,6},{6,5},{9,10},{10,9},{13,14},{14,13},{17,18},{18,... | collective-permute-start | bytes 12296 | tf_op jit(solution)/shard_map/ppermute | solution.py:231
  66.2 32.4 %collective-permute-start.11 = (f32[8,128]{1,0:T(8,128)S(1)}, f32[8,128]{1,0:T(8,128)S(1)}, u32[]{:S(2)}, u32[]{:S(2)}) collective-permute-start(f32[8,128]{1,0:T(8,128)S(1)} %get-tuple-element.39.own), channel_id=1, source_target_pairs={{1,0},{2,3},{5,4},{6,7},{9,8},{10,11},{13,12},{14,15},{17,16},{18,... | collective-permute-start | bytes 12296 | tf_op jit(solution)/shard_map/ppermute | solution.py:231
  67.5 32.8 %collective-permute-start.12 = (f32[8,128]{1,0:T(8,128)S(1)}, f32[8,128]{1,0:T(8,128)S(1)}, u32[]{:S(2)}, u32[]{:S(2)}) collective-permute-start(f32[8,128]{1,0:T(8,128)S(1)} %get-tuple-element.39.own), channel_id=1, source_target_pairs={{1,3},{2,0},{5,7},{6,4},{9,11},{10,8},{13,15},{14,12},{17,19},{18,... | collective-permute-start | bytes 12296 | tf_op jit(solution)/shard_map/ppermute | solution.py:231
where the time goes:
time: 102 us
  Pallas kernels  43.2 us (42%)
  waiting for transfers between devices  35.6 us (35%)
  starting transfers between devices  20.1 us (20%)
  local copies, waits for them, and re-layouts  1.75 us (2%)
    ppermute x13, waiting for transfers between devices, on_line(): send = lambda x, pairs: lax.ppermute(x, 'bond', pairs)  35.6 us
    pallas_call x3, Pallas kernels, level(): pl.pallas_call(functools.partial(level_kernel, len(pieces), section > 0,...  22.5 us
    ppermute x13, starting transfers between devices, on_line(): send = lambda x, pairs: lax.ppermute(x, 'bond', pairs)  20.1 us
    pallas_call x3, Pallas kernels, more(): pl.pallas_call(functools.partial(more_kernel, wired, rows, width), out_sh...  19.9 us
  transfers between devices with their start and end apart: 13, of which 4 were waited for; matrix products, arithmetic and copies ran while one was open for 1% of the time, Pallas kernels for 20%

commit v1 on v0

--- a/solution.py
+++ b/solution.py
@@ -35,12 +35,14 @@
     pairs = width // 2
     groups = pairs // 4
     cells = width * width
-    low_half = lax.broadcasted_iota(jnp.int32, (pairs, LANES), 1) < width
+    batch = min(rows, 8)
+    low_half = lax.broadcasted_iota(jnp.int32, (width, LANES), 1) < width
+    low_few = lax.broadcasted_iota(jnp.int32, (pairs, LANES), 1) < width
 
     def first(q, g):
         blocks = []
-        for n in range(4):
-            at = pl.multiple_of((4 * q + n) * PITCH, 8)
+        for n in range(batch):
+            at = pl.multiple_of((batch * q + n) * PITCH, 8)
             highs = spread[pl.ds(at, width), :]
             lows = spread[pl.ds(rows * PITCH + at, width), :]
             blocks.append(jnp.concatenate([highs, lows[:, :width]], axis=1))
@@ -48,32 +50,38 @@
         return jnp.dot(u, stacked[:, g * 512 : (g + 1) * 512], preferred_element_type=F32)
 
     def second(inner, g):
-        high = inner.astype(BF16)
-        low = (inner - high.astype(F32)).astype(BF16)
-
-        def block(array, i):
-            return jnp.concatenate(
-                [array[n * width : (n + 1) * width, i * LANES : (i + 1) * LANES] for n in range(4)],
-                axis=1,
-            )
-
-        highs = [block(high, i) for i in range(4)]
-        lows = [block(low, i) for i in range(4)]
-        weights = jnp.concatenate([h for h in highs for _ in range(2)] + lows, axis=0)
-        return jnp.dot(
-            factor[:, g * 768 : (g + 1) * 768], weights, preferred_element_type=F32
+        strips = []
+        for i in range(4):
+            evens, odds = [], []
+            for n in range(0, batch, 2):
+                lanes = slice(i * LANES, (i + 1) * LANES)
+                one = inner[n * width : (n + 1) * width, lanes]
+                two = inner[(n + 1) * width : (n + 2) * width, lanes]
+                kept = jnp.where(low_half, one, two)
+                moved = pltpu.roll(jnp.where(low_half, two, one), width, 1)
+                evens.append(jnp.where(low_half, kept, moved))
+                odds.append(jnp.where(low_half, moved, kept))
+            strips += [jnp.concatenate(evens, axis=1), jnp.concatenate(odds, axis=1)]
+        weights = jnp.concatenate(strips, axis=0)
+        high = weights.astype(BF16)
+        low = (weights - high.astype(F32)).astype(BF16)
+        left = factor[:, g * 512 : (g + 1) * 512]
+        return (
+            jnp.dot(left, high, preferred_element_type=F32),
+            jnp.dot(left[:width], low, preferred_element_type=F32),
         )
 
-    def finish_quad(q, total, peak):
-        for n in range(4):
-            part = total[:, n * LANES : (n + 1) * LANES]
-            even0, odd0, even1, odd1 = (part[r * pairs : (r + 1) * pairs] for r in range(4))
-            kept = jnp.where(low_half, even0, odd1)
-            moved = jnp.where(low_half, odd0, even1)
-            value = kept + pltpu.roll(moved, width, 1)
-            peak = jnp.maximum(peak, jnp.abs(value))
-            at = (q // 2) * (8 * pairs) + (q % 2) * 4 + n
-            placed[pl.ds(at, pairs, stride=8), :] = value
+    def finish_batch(q, total, peak):
+        total = total[0][:width] + (total[0][width:] + total[1])
+        for n in range(0, batch, 2):
+            part = total[:, n // 2 * LANES : (n // 2 + 1) * LANES]
+            even, odd = part[:pairs], part[pairs:]
+            for r, value in (
+                (n, jnp.where(low_few, even, pltpu.roll(odd, width, 1))),
+                (n + 1, jnp.where(low_few, pltpu.roll(even, width, 1), odd)),
+            ):
+                peak = jnp.maximum(peak, jnp.abs(value))
+                placed[pl.ds(q * (8 * pairs) + r, pairs, stride=8), :] = value
         return peak
 
     def several(count, start, peak):
@@ -83,16 +91,14 @@
         for k, (q, g) in enumerate(steps):
             ahead = first(*steps[k + 1]) if k + 1 < len(steps) else None
             update = second(inner, g)
-            total = update if g == 0 else total + update
+            total = update if g == 0 else (total[0] + update[0], total[1] + update[1])
             if g + 1 == groups:
-                peak = finish_quad(q, total, peak)
+                peak = finish_batch(q, total, peak)
             inner = ahead
         return peak
 
     peak = jnp.zeros((pairs, LANES), F32)
-    quads = rows // 4
-    each = 2 if quads % 2 == 0 else 1
-    peak = lax.fori_loop(0, quads // each, lambda i, p: several(each, i * each, p), peak)
+    peak = lax.fori_loop(0, rows // batch, lambda i, p: several(1, i, p), peak)
     highest = jnp.max(peak)
     tall = min(rows, 8)
     for h in range(rows // tall):
@@ -142,19 +148,15 @@
         turned[pl.ds(x, width, stride=PITCH), :] = both[:width]
         turned[pl.ds(pairs + x, width, stride=PITCH), :] = both[width:]
 
-    groups = pairs // 4
-    for g in range(groups):
-        blocks = []
-        for i in range(4):
-            b = 2 * (4 * g + i)
-            upper = turned[b * PITCH : b * PITCH + width, :].astype(BF16)
-            lower = turned[(b + 1) * PITCH : (b + 1) * PITCH + width, :].astype(BF16)
-            blocks.append(jnp.concatenate([upper, lower], axis=0))
-        highs = [
-            jnp.concatenate([blocks[i][:, :width], blocks[i + 1][:, :width]], axis=1)
-            for i in (0, 2)
-        ]
-        factor[:, g * 768 : (g + 1) * 768] = jnp.concatenate(blocks + highs, axis=1)
+    low_half = lax.broadcasted_iota(jnp.int32, (width, LANES), 1) < width
+    for x in range(pairs):
+        one = turned[2 * x * PITCH : 2 * x * PITCH + width, :]
+        two = turned[(2 * x + 1) * PITCH : (2 * x + 1) * PITCH + width, :]
+        lanes = slice(x * LANES, (x + 1) * LANES)
+        kept = jnp.where(low_half, one, two)
+        moved = pltpu.roll(jnp.where(low_half, two, one), width, 1)
+        factor[0:width, lanes] = jnp.where(low_half, kept, moved).astype(BF16)
+        factor[width:, lanes] = jnp.where(low_half, moved, kept).astype(BF16)
 
     highest = contract(rows, width, wired, stacked, factor, u_ref, out_ref, placed, spread)
     notes_ref[0:4, :] = jnp.full((4, LANES), highest, F32)
@@ -188,7 +190,7 @@
             jax.ShapeDtypeStruct((rows, span), F32),
             jax.ShapeDtypeStruct((8, LANES), F32),
             jax.ShapeDtypeStruct((3 * width, cells), BF16),
-            jax.ShapeDtypeStruct((2 * width, 96 * width), BF16),
+            jax.ShapeDtypeStruct((2 * width, cells), BF16),
         ],
         scratch_shapes=[
             pltpu.VMEM((width, cells), F32),
@@ -230,8 +232,8 @@
     sections = isometries.shape[0]
     send = lambda x, pairs: lax.ppermute(x, "bond", pairs)
     inward, swap, outward = [(0, 1), (3, 2)], [(1, 2), (2, 1)], [(1, 0), (2, 3)]
+    near = send(tensor, inward)
     far = send(tensor, [(0, 2), (3, 1)])
-    near = send(tensor, inward)
     other = send(tensor, swap)
     pieces = [tensor, near, other, far]
     theirs = [send(isometries[0], inward)]
@@ -258,7 +260,11 @@
         functools.partial(line_finish_kernel, sections),
         out_shape=[
             jax.ShapeDtypeStruct(tensor.shape, F32),
-            jax.ShapeDtypeStruct((8, LANES), F32),
+            jax.ShapeDtypeStruct((1, 1), F32),
+        ],
+        out_specs=[
+            pl.BlockSpec(memory_space=pltpu.VMEM),
+            pl.BlockSpec(memory_space=pltpu.SMEM),
         ],
         compiler_params=params(),
         name="finish",
@@ -272,8 +278,7 @@
     def write(value_ref, one, two):
         largest = jnp.maximum(one[0:4, :], two[0:4, :]) + EPSILON
         log_density = one[4:8, :] + jnp.log(largest) * 0.5**sections
-        log_ref[0:4, :] = log_density
-        log_ref[4:8, :] = log_density
+        log_ref[0, 0] = jnp.max(log_density)
         out_ref[...] = value_ref[...] / largest[0:1, 0:1]
 
     @pl.when(inner)
@@ -306,7 +311,7 @@
 def on_device(tensor, isometries):
     if lax.axis_size("bond") == 4:
         final, log_density = on_line(tensor, isometries)
-        return final, log_density[0, :1]
+        return final, log_density.reshape(1)
     return gathered(tensor, isometries)
 
 

time: 102 us -> 99.8 us (0.978)
  Pallas kernels: 43.2 us -> 41.3 us
    pallas_call x3, Pallas kernels: 19.9 us -> 18.9 us  [more(): pl.pallas_call(functools.partial(more_kernel, wired, rows, width), out_sh...]
where the time goes in v1:
time: 99.8 us; the launch traced here: 99.4 us
  Pallas kernels  41.3 us (41%)
  waiting for transfers between devices  35.6 us (36%)
  starting transfers between devices  20.1 us (20%)
  local copies, waits for them, and re-layouts  1.24 us (1%)
  between operations  1.06 us (1%)
    ppermute x13, waiting for transfers between devices, on_line(): send = lambda x, pairs: lax.ppermute(x, 'bond', pairs)  35.6 us
    pallas_call x3, Pallas kernels, level(): pl.pallas_call(functools.partial(level_kernel, len(pieces), section > 0,...  21.6 us
    ppermute x13, starting transfers between devices, on_line(): send = lambda x, pairs: lax.ppermute(x, 'bond', pairs)  20.1 us
    pallas_call x3, Pallas kernels, more(): pl.pallas_call(functools.partial(more_kernel, wired, rows, width), out_sh...  18.9 us
  transfers between devices with their start and end apart: 13, of which 4 were waited for; matrix products, arithmetic and copies ran while one was open for 1% of the time, Pallas kernels for 20%

profile of v1, /device:TPU:0, one launch (start us, length us, event | category | flops | bytes accessed | tf_op | source)
XLA Modules:
  0.0 99.4 jit_solution(13165796484243244101)
XLA Ops:
  0.6 5.1 %collective-permute-start = (f32[16,4096]{1,0:T(8,128)}, f32[16,4096]{1,0:T(8,128)S(1)}, u32[]{:S(2)}, u32[]{:S(2)}) collective-permute-start(f32[16,4096]{1,0:T(8,128)} %refs_0_.1), channel_id=1, source_target_pairs={{0,1},{3,2},{4,5},{7,6},{8,9},{11,10},{12,13},{15,14},{16,17},{19,... | collective-permute-start | bytes 786440 | tf_op jit(solution)/shard_map/ppermute | solution.py:233
  5.8 0.7 collective-permute-start.1
  6.4 4.0 %collective-permute-start.2 = (f32[16,4096]{1,0:T(8,128)}, f32[16,4096]{1,0:T(8,128)S(1)}, u32[]{:S(2)}, u32[]{:S(2)}) collective-permute-start(f32[16,4096]{1,0:T(8,128)} %refs_0_.1), channel_id=1, source_target_pairs={{0,2},{3,1},{4,6},{7,5},{8,10},{11,9},{12,14},{15,13},{16,18},{19,... | collective-permute-start | bytes 786440 | tf_op jit(solution)/shard_map/ppermute | solution.py:233
  10.4 1.2 %slice_bitcast_fusion.2 = (f32[16,4096]{1,0:T(8,128)S(1)}, f32[16,4096]{1,0:T(8,128)S(1)}, f32[16,4096]{1,0:T(8,128)S(1)}) fusion(f32[3,16,4096]{2,1,0:T(8,128)} %param.3), kind=kLoop, calls=%fused_computation.2 | loop fusion | bytes 1572864 | tf_op jit(solution)/shard_map/squeeze | solution.py:245
  11.6 1.4 %collective-permute-start.3 = (f32[16,4096]{1,0:T(8,128)S(1)}, f32[16,4096]{1,0:T(8,128)S(1)}, u32[]{:S(2)}, u32[]{:S(2)}) collective-permute-start(f32[16,4096]{1,0:T(8,128)S(1)} %get-tuple-element.44.refs_4_), channel_id=1, source_target_pairs={{0,1},{3,2},{4,5},{7,6},{8,9},{11,10},{12,13},{15,14},{16,17},{19,... | collective-permute-start | bytes 786440 | tf_op jit(solution)/shard_map/ppermute | solution.py:233
  13.1 1.3 %collective-permute-start.6 = (f32[2,16,4096]{2,1,0:T(8,128)S(1)}, f32[2,16,4096]{2,1,0:T(8,128)S(1)}, u32[]{:S(2)}, u32[]{:S(2)}) collective-permute-start(f32[2,16,4096]{2,1,0:T(8,128)S(1)} %slice.21), channel_id=1, source_target_pairs={{0,1},{3,2},{4,5},{7,6},{8,9},{11,10},{12,13},{15,14},{16,17},{19,... | collective-permute-start | bytes 1572872 | tf_op jit(solution)/shard_map/ppermute | solution.py:233
  14.4 0.0 collective-permute-done.refs_1_
  14.4 0.0 collective-permute-done.1.refs_2_
  14.4 4.0 %collective-permute-done.2.refs_3_ = f32[16,4096]{1,0:T(8,128)S(1)} collective-permute-done((f32[16,4096]{1,0:T(8,128)}, f32[16,4096]{1,0:T(8,128)S(1)}, u32[]{:S(2)}, u32[]{:S(2)}) %collective-permute-start.2) | collective-permute-done | bytes 262176 | tf_op jit(solution)/shard_map/ppermute | solution.py:233
  18.4 7.0 %level.3 = (f32[16,4224]{1,0:T(8,128)S(1)}, f32[8,128]{1,0:T(8,128)S(1)}, bf16[192,4096]{1,0:T(8,128)(2,1)S(1)}, bf16[128,4096]{1,0:T(8,128)(2,1)S(1)}) custom-call(f32[16,4096]{1,0:T(8,128)S(1)} %copy-done, f32[16,4096]{1,0:T(8,128)S(1)} %collective-permute-done.refs_1_, f32[16,4096]{1,0:T(8,128)S(1)} %collective-permute-done.1.refs_2_, ...), custom_call_target="tpu_custom_call" | custom-call | flops 3221225472 | bytes 4194304 | tf_op jit(solution)/shard_map/level/pallas_call | solution.py:185
  25.5 0.0 collective-permute-done.3.u_ref
  25.5 6.2 %more.3 = (f32[16,4224]{1,0:T(8,128)S(1)}, f32[8,128]{1,0:T(8,128)S(1)}) custom-call(bf16[192,4096]{1,0:T(8,128)(2,1)S(1)} %get-tuple-element.23.stacked, bf16[128,4096]{1,0:T(8,128)(2,1)S(1)} %get-tuple-element.24.factor, f32[16,4096]{1,0:T(8,128)S(1)} %collective-permute-done.3.u_ref, f32[8,128]{1,0:T(8,128)S(1)} %get-tuple-element.25.before_ref), custom_call_target="tpu_custom_call" | custom-call | flops 3221225472 | bytes 4194304 | tf_op jit(solution)/shard_map/more/pallas_call | solution.py:211
  31.7 0.7 collective-permute-start.5
  32.4 0.9 collective-permute-start.4
  33.2 0.8 collective-permute-done.6
  34.1 0.0 collective-permute-done.5.refs_3_
  34.1 0.0 collective-permute-done.4.refs_2_
  34.1 7.2 %level.4 = (f32[16,4224]{1,0:T(8,128)S(1)}, f32[8,128]{1,0:T(8,128)S(1)}, bf16[192,4096]{1,0:T(8,128)(2,1)S(1)}, bf16[128,4096]{1,0:T(8,128)(2,1)S(1)}) custom-call(f32[16,4224]{1,0:T(8,128)S(1)} %get-tuple-element.22.refs_0_, f32[16,4224]{1,0:T(8,128)S(1)} %get-tuple-element.26.refs_1_, f32[16,4224]{1,0:T(8,128)S(1)} %collective-permute-done.4.refs_2_, ...), custom_call_target="tpu_custom_call" | custom-call | flops 3221225472 | bytes 4194304 | tf_op jit(solution)/shard_map/level/pallas_call | solution.py:185
  41.3 6.3 %more.4 = (f32[16,4224]{1,0:T(8,128)S(1)}, f32[8,128]{1,0:T(8,128)S(1)}) custom-call(bf16[192,4096]{1,0:T(8,128)(2,1)S(1)} %get-tuple-element.29.stacked, bf16[128,4096]{1,0:T(8,128)(2,1)S(1)} %get-tuple-element.30.factor, f32[16,4096]{1,0:T(8,128)S(1)} %get-tuple-element.46.u_ref, f32[8,128]{1,0:T(8,128)S(1)} %get-tuple-element.31.before_ref), custom_call_target="tpu_custom_call" | custom-call | flops 3221225472 | bytes 4194304 | tf_op jit(solution)/shard_map/more/pallas_call | solution.py:211
  47.6 0.7 collective-permute-start.8
  48.3 0.7 collective-permute-start.7
  49.0 0.0 collective-permute-done.8.refs_3_
  49.0 0.0 collective-permute-done.7.refs_2_
  49.0 7.3 %level.5 = (f32[16,4096]{1,0:T(8,128)S(1)}, f32[8,128]{1,0:T(8,128)S(1)}, bf16[192,4096]{1,0:T(8,128)(2,1)S(1)}, bf16[128,4096]{1,0:T(8,128)(2,1)S(1)}) custom-call(f32[16,4224]{1,0:T(8,128)S(1)} %get-tuple-element.28.refs_0_, f32[16,4224]{1,0:T(8,128)S(1)} %get-tuple-element.32.refs_1_, f32[16,4224]{1,0:T(8,128)S(1)} %collective-permute-done.7.refs_2_, ...), custom_call_target="tpu_custom_call" | custom-call | flops 3221225472 | bytes 4194304 | tf_op jit(solution)/shard_map/level/pallas_call | solution.py:185
  56.3 1.5 %collective-permute-start.9 = (f32[16,4096]{1,0:T(8,128)S(1)}, f32[16,4096]{1,0:T(8,128)S(1)}, u32[]{:S(2)}, u32[]{:S(2)}) collective-permute-start(f32[16,4096]{1,0:T(8,128)S(1)} %get-tuple-element.38), channel_id=1, source_target_pairs={{1,0},{2,3},{5,4},{6,7},{9,8},{10,11},{13,12},{14,15},{17,16},{18,... | collective-permute-start | bytes 786440 | tf_op jit(solution)/shard_map/ppermute | solution.py:233
  57.8 6.4 %more.5 = (f32[16,4096]{1,0:T(8,128)S(1)}, f32[8,128]{1,0:T(8,128)S(1)}) custom-call(bf16[192,4096]{1,0:T(8,128)(2,1)S(1)} %get-tuple-element.34.stacked, bf16[128,4096]{1,0:T(8,128)(2,1)S(1)} %get-tuple-element.35.factor, f32[16,4096]{1,0:T(8,128)S(1)} %get-tuple-element.42.u_ref, f32[8,128]{1,0:T(8,128)S(1)} %get-tuple-element.36.before_ref), custom_call_target="tpu_custom_call" | custom-call | flops 3221225472 | bytes 4194304 | tf_op jit(solution)/shard_map/more/pallas_call | solution.py:211
  64.2 0.7 collective-permute-start.10
  64.9 1.3 %collective-permute-start.11 = (f32[8,128]{1,0:T(8,128)S(1)}, f32[8,128]{1,0:T(8,128)S(1)}, u32[]{:S(2)}, u32[]{:S(2)}) collective-permute-start(f32[8,128]{1,0:T(8,128)S(1)} %get-tuple-element.39.own), channel_id=1, source_target_pairs={{1,0},{2,3},{5,4},{6,7},{9,8},{10,11},{13,12},{14,15},{17,16},{18,... | collective-permute-start | bytes 12296 | tf_op jit(solution)/shard_map/ppermute | solution.py:233
  66.2 1.3 %collective-permute-start.12 = (f32[8,128]{1,0:T(8,128)S(1)}, f32[8,128]{1,0:T(8,128)S(1)}, u32[]{:S(2)}, u32[]{:S(2)}) collective-permute-start(f32[8,128]{1,0:T(8,128)S(1)} %get-tuple-element.39.own), channel_id=1, source_target_pairs={{1,3},{2,0},{5,7},{6,4},{9,11},{10,8},{13,15},{14,12},{17,19},{18,... | collective-permute-start | bytes 12296 | tf_op jit(solution)/shard_map/ppermute | solution.py:233
  67.5 29.3 %collective-permute-done.11.near = f32[8,128]{1,0:T(8,128)S(1)} collective-permute-done((f32[8,128]{1,0:T(8,128)S(1)}, f32[8,128]{1,0:T(8,128)S(1)}, u32[]{:S(2)}, u32[]{:S(2)}) %collective-permute-start.11) | collective-permute-done | bytes 4128 | tf_op jit(solution)/shard_map/ppermute | solution.py:233
  96.8 1.6 %collective-permute-done.12.far = f32[8,128]{1,0:T(8,128)S(1)} collective-permute-done((f32[8,128]{1,0:T(8,128)S(1)}, f32[8,128]{1,0:T(8,128)S(1)}, u32[]{:S(2)}, u32[]{:S(2)}) %collective-permute-start.12) | collective-permute-done | bytes 4128 | tf_op jit(solution)/shard_map/ppermute | solution.py:233
  98.4 0.9 finish.1
  (9 shorter events, 0.1 us)
Async XLA Ops:
  0.6 17.8 %copy-start = (f32[16,4096]{1,0:T(8,128)S(1)}, f32[16,4096]{1,0:T(8,128)}, u32[]{:S(2)}) copy-start(f32[16,4096]{1,0:T(8,128)} %refs_0_.1) | copy-start | bytes 786436
  0.6 12.4 %copy-start.1 = (f32[3,16,4096]{2,1,0:T(8,128)S(1)}, f32[3,16,4096]{2,1,0:T(8,128)}, u32[]{:S(2)}) copy-start(f32[3,16,4096]{2,1,0:T(8,128)} %param.3) | copy-start | bytes 2359300
  0.6 13.8 %collective-permute-start = (f32[16,4096]{1,0:T(8,128)}, f32[16,4096]{1,0:T(8,128)S(1)}, u32[]{:S(2)}, u32[]{:S(2)}) collective-permute-start(f32[16,4096]{1,0:T(8,128)} %refs_0_.1), channel_id=1, source_target_pairs={{0,1},{3,2},{4,5},{7,6},{8,9},{11,10},{12,13},{15,14},{16,17},{19,... | collective-permute-start | bytes 786440 | tf_op jit(solution)/shard_map/ppermute | solution.py:233
  5.8 8.7 %collective-permute-start.1 = (f32[16,4096]{1,0:T(8,128)}, f32[16,4096]{1,0:T(8,128)S(1)}, u32[]{:S(2)}, u32[]{:S(2)}) collective-permute-start(f32[16,4096]{1,0:T(8,128)} %refs_0_.1), channel_id=1, source_target_pairs={{1,2},{2,1},{5,6},{6,5},{9,10},{10,9},{13,14},{14,13},{17,18},{18,... | collective-permute-start | bytes 786440 | tf_op jit(solution)/shard_map/ppermute | solution.py:233
  6.4 12.0 %collective-permute-start.2 = (f32[16,4096]{1,0:T(8,128)}, f32[16,4096]{1,0:T(8,128)S(1)}, u32[]{:S(2)}, u32[]{:S(2)}) collective-permute-start(f32[16,4096]{1,0:T(8,128)} %refs_0_.1), channel_id=1, source_target_pairs={{0,2},{3,1},{4,6},{7,5},{8,10},{11,9},{12,14},{15,13},{16,18},{19,... | collective-permute-start | bytes 786440 | tf_op jit(solution)/shard_map/ppermute | solution.py:233
  11.6 13.9 %collective-permute-start.3 = (f32[16,4096]{1,0:T(8,128)S(1)}, f32[16,4096]{1,0:T(8,128)S(1)}, u32[]{:S(2)}, u32[]{:S(2)}) collective-permute-start(f32[16,4096]{1,0:T(8,128)S(1)} %get-tuple-element.44.refs_4_), channel_id=1, source_target_pairs={{0,1},{3,2},{4,5},{7,6},{8,9},{11,10},{12,13},{15,14},{16,17},{19,... | collective-permute-start | bytes 786440 | tf_op jit(solution)/shard_map/ppermute | solution.py:233
  13.1 20.9 %collective-permute-start.6 = (f32[2,16,4096]{2,1,0:T(8,128)S(1)}, f32[2,16,4096]{2,1,0:T(8,128)S(1)}, u32[]{:S(2)}, u32[]{:S(2)}) collective-permute-start(f32[2,16,4096]{2,1,0:T(8,128)S(1)} %slice.21), channel_id=1, source_target_pairs={{0,1},{3,2},{4,5},{7,6},{8,9},{11,10},{12,13},{15,14},{16,17},{19,... | collective-permute-start | bytes 1572872 | tf_op jit(solution)/shard_map/ppermute | solution.py:233
  31.7 2.4 %collective-permute-start.5 = (f32[16,4224]{1,0:T(8,128)S(1)}, f32[16,4224]{1,0:T(8,128)S(1)}, u32[]{:S(2)}, u32[]{:S(2)}) collective-permute-start(f32[16,4224]{1,0:T(8,128)S(1)} %get-tuple-element.26.refs_1_), channel_id=1, source_target_pairs={{1,2},{2,1},{5,6},{6,5},{9,10},{10,9},{13,14},{14,13},{17,18},{18,... | collective-permute-start | bytes 811016 | tf_op jit(solution)/shard_map/ppermute | solution.py:233
  32.4 1.7 %collective-permute-start.4 = (f32[16,4224]{1,0:T(8,128)S(1)}, f32[16,4224]{1,0:T(8,128)S(1)}, u32[]{:S(2)}, u32[]{:S(2)}) collective-permute-start(f32[16,4224]{1,0:T(8,128)S(1)} %get-tuple-element.22.refs_0_), channel_id=1, source_target_pairs={{1,2},{2,1},{5,6},{6,5},{9,10},{10,9},{13,14},{14,13},{17,18},{18,... | collective-permute-start | bytes 811016 | tf_op jit(solution)/shard_map/ppermute | solution.py:233
  47.6 1.4 %collective-permute-start.8 = (f32[16,4224]{1,0:T(8,128)S(1)}, f32[16,4224]{1,0:T(8,128)S(1)}, u32[]{:S(2)}, u32[]{:S(2)}) collective-permute-start(f32[16,4224]{1,0:T(8,128)S(1)} %get-tuple-element.32.refs_1_), channel_id=1, source_target_pairs={{1,2},{2,1},{5,6},{6,5},{9,10},{10,9},{13,14},{14,13},{17,18},{18,... | collective-permute-start | bytes 811016 | tf_op jit(solution)/shard_map/ppermute | solution.py:233
  48.3 0.7 collective-permute-start.7
  56.3 42.0 %collective-permute-start.9 = (f32[16,4096]{1,0:T(8,128)S(1)}, f32[16,4096]{1,0:T(8,128)S(1)}, u32[]{:S(2)}, u32[]{:S(2)}) collective-permute-start(f32[16,4096]{1,0:T(8,128)S(1)} %get-tuple-element.38), channel_id=1, source_target_pairs={{1,0},{2,3},{5,4},{6,7},{9,8},{10,11},{13,12},{14,15},{17,16},{18,... | collective-permute-start | bytes 786440 | tf_op jit(solution)/shard_map/ppermute | solution.py:233
  64.2 3.3 %collective-permute-start.10 = (f32[8,128]{1,0:T(8,128)S(1)}, f32[8,128]{1,0:T(8,128)S(1)}, u32[]{:S(2)}, u32[]{:S(2)}) collective-permute-start(f32[8,128]{1,0:T(8,128)S(1)} %get-tuple-element.39.own), channel_id=1, source_target_pairs={{1,2},{2,1},{5,6},{6,5},{9,10},{10,9},{13,14},{14,13},{17,18},{18,... | collective-permute-start | bytes 12296 | tf_op jit(solution)/shard_map/ppermute | solution.py:233
  64.9 31.9 %collective-permute-start.11 = (f32[8,128]{1,0:T(8,128)S(1)}, f32[8,128]{1,0:T(8,128)S(1)}, u32[]{:S(2)}, u32[]{:S(2)}) collective-permute-start(f32[8,128]{1,0:T(8,128)S(1)} %get-tuple-element.39.own), channel_id=1, source_target_pairs={{1,0},{2,3},{5,4},{6,7},{9,8},{10,11},{13,12},{14,15},{17,16},{18,... | collective-permute-start | bytes 12296 | tf_op jit(solution)/shard_map/ppermute | solution.py:233
  66.2 32.2 %collective-permute-start.12 = (f32[8,128]{1,0:T(8,128)S(1)}, f32[8,128]{1,0:T(8,128)S(1)}, u32[]{:S(2)}, u32[]{:S(2)}) collective-permute-start(f32[8,128]{1,0:T(8,128)S(1)} %get-tuple-element.39.own), channel_id=1, source_target_pairs={{1,3},{2,0},{5,7},{6,4},{9,11},{10,8},{13,15},{14,12},{17,19},{18,... | collective-permute-start | bytes 12296 | tf_op jit(solution)/shard_map/ppermute | solution.py:233

commit v2 on v1

--- a/solution.py
+++ b/solution.py
@@ -110,13 +110,13 @@
     return highest
 
 
-def level_kernel(count, scaled, section, wired, rows, width, sources, *refs):
-    pieces = refs[:count]
-    u_ref, before_ref, out_ref, notes_ref, stacked, factor = refs[count : count + 6]
-    whole, turned, placed, spread = refs[count + 6 :]
+def split_tensor(
+    pieces, scaled, section, width, sources, before_ref, notes_ref, stacked, factor, whole, turned
+):
     held = pieces[0].shape[0]
     pairs = width // 2
     cells = width * width
+    count = len(pieces)
     found = sources(lax.axis_index("bond"))
     log_density = before_ref[4:8, :]
     inverse = None
@@ -158,9 +158,30 @@
         factor[0:width, lanes] = jnp.where(low_half, kept, moved).astype(BF16)
         factor[width:, lanes] = jnp.where(low_half, moved, kept).astype(BF16)
 
+    notes_ref[4:8, :] = log_density
+
+
+def level_kernel(count, scaled, section, wired, rows, width, sources, *refs):
+    pieces = refs[:count]
+    u_ref, before_ref, out_ref, notes_ref, stacked, factor = refs[count : count + 6]
+    whole, turned, placed, spread = refs[count + 6 :]
+    split_tensor(
+        pieces, scaled, section, width, sources, before_ref, notes_ref, stacked, factor, whole, turned
+    )
     highest = contract(rows, width, wired, stacked, factor, u_ref, out_ref, placed, spread)
     notes_ref[0:4, :] = jnp.full((4, LANES), highest, F32)
-    notes_ref[4:8, :] = log_density
+
+
+def last_kernel(count, section, rows, width, sources, *refs):
+    pieces = refs[:count]
+    end_u_ref, u_ref, before_ref, end_out_ref, out_ref, notes_ref = refs[count : count + 6]
+    stacked, factor, whole, turned, placed, spread = refs[count + 6 :]
+    cells = width * width
+    split_tensor(pieces, True, section, width, sources, before_ref, notes_ref, stacked, factor, whole, turned)
+    one = contract(rows, width, False, stacked, factor, end_u_ref, end_out_ref, placed, spread)
+    two = contract(rows, width, False, stacked, factor, u_ref, out_ref, placed, spread)
+    notes_ref[0:4, :] = jnp.full((4, LANES), jnp.maximum(one, two), F32)
+    end_out_ref[0:8, cells:] = notes_ref[...]
 
 
 def more_kernel(wired, rows, width, stacked, factor, u_ref, before_ref, out_ref, notes_ref, placed, spread):
@@ -204,6 +225,30 @@
     )(*pieces, isometry, notes)
 
 
+def last_level(pieces, sources, end_isometry, isometry, notes, section):
+    width = sum(piece.shape[0] for piece in pieces)
+    rows, cells = isometry.shape
+    return pl.pallas_call(
+        functools.partial(last_kernel, len(pieces), section, rows, width, sources),
+        out_shape=[
+            jax.ShapeDtypeStruct((rows, cells + LANES), F32),
+            jax.ShapeDtypeStruct((rows, cells), F32),
+            jax.ShapeDtypeStruct((8, LANES), F32),
+        ],
+        scratch_shapes=[
+            pltpu.VMEM((3 * width, cells), BF16),
+            pltpu.VMEM((2 * width, cells), BF16),
+            pltpu.VMEM((width, cells), F32),
+            pltpu.VMEM((width * PITCH, LANES), F32),
+            pltpu.VMEM((max(rows, 8) * width // 2, LANES), F32),
+            pltpu.VMEM((2 * rows * PITCH, LANES), F32),
+        ],
+        compiler_params=params(),
+        cost_estimate=cost(2 * rows, width),
+        name="last",
+    )(*pieces, end_isometry, isometry, notes)
+
+
 def more(stacked, factor, isometry, notes, wired):
     width = stacked.shape[0] // 3
     rows, cells = isometry.shape
@@ -240,22 +285,20 @@
     later = send(isometries[1:], inward)
     theirs += [later[k] for k in range(sections - 1)]
     notes = jnp.zeros((8, LANES), F32)
-    for section in range(sections):
-        last = section + 1 == sections
-        mine = isometries[section]
-        order = [theirs[section], mine] if last else [mine, theirs[section]]
+    for section in range(sections - 1):
         first, notes, stacked, factor = level(
-            pieces, middle_sources, order[0], notes, section, not last
+            pieces, middle_sources, isometries[section], notes, section, True
         )
-        if last:
-            break
         first_other = send(first, swap)
-        second, notes = more(stacked, factor, order[1], notes, True)
+        second, notes = more(stacked, factor, theirs[section], notes, True)
         second_other = send(second, swap)
         pieces = [first, second, first_other, second_other]
-    moved = send(first, outward)
-    second, notes = more(stacked, factor, order[1], notes, False)
-    found = [notes, send(notes, swap), send(notes, outward), send(notes, [(1, 3), (2, 0)])]
+    moved, own, notes = last_level(
+        pieces, middle_sources, theirs[-1], isometries[sections - 1], notes, sections - 1
+    )
+    moved = send(moved, outward)
+    across = send(notes, [(1, 3), (2, 0)])
+    swapped = send(notes, swap)
     return pl.pallas_call(
         functools.partial(line_finish_kernel, sections),
         out_shape=[
@@ -268,26 +311,26 @@
         ],
         compiler_params=params(),
         name="finish",
-    )(second, moved, *found)
-
-
-def line_finish_kernel(sections, second_ref, moved_ref, own, swapped, near, far, out_ref, log_ref):
+    )(own, moved, notes, swapped, across)
+
+
+def line_finish_kernel(sections, own_ref, moved_ref, notes, swapped, across, out_ref, log_ref):
     me = lax.axis_index("bond")
     inner = jnp.logical_or(me == 1, me == 2)
+    cells = own_ref.shape[1]
 
     def write(value_ref, one, two):
         largest = jnp.maximum(one[0:4, :], two[0:4, :]) + EPSILON
-        log_density = one[4:8, :] + jnp.log(largest) * 0.5**sections
-        log_ref[0, 0] = jnp.max(log_density)
-        out_ref[...] = value_ref[...] / largest[0:1, 0:1]
+        log_ref[0, 0] = jnp.max(one[4:8, :] + jnp.log(largest) * 0.5**sections)
+        out_ref[...] = value_ref[:, :cells] / largest[0:1, 0:1]
 
     @pl.when(inner)
     def _():
-        write(second_ref, own, swapped)
+        write(own_ref, notes[...], swapped)
 
     @pl.when(jnp.logical_not(inner))
     def _():
-        write(moved_ref, near, far)
+        write(moved_ref, moved_ref[0:8, cells:], across)
 
 
 def gathered(tensor, isometries):

time: 99.8 us -> 98.1 us (0.983)
  starting transfers between devices: 20.1 us -> 18.9 us
    pallas_call x0 -> x1, Pallas kernels: none -> 13.3 us  [last_level(): pl.pallas_call(functools.partial(last_kernel, len(pieces), section, rows,...]
    pallas_call x3 -> x2, Pallas kernels: 21.6 us -> 14.4 us  [level(): pl.pallas_call(functools.partial(level_kernel, len(pieces), section > 0,...]
    pallas_call x3 -> x2, Pallas kernels: 18.9 us -> 12.6 us  [more(): pl.pallas_call(functools.partial(more_kernel, wired, rows, width), out_sh...]
    ppermute x13 -> x12, starting transfers between devices: 20.1 us -> 18.9 us  [on_line(): send = lambda x, pairs: lax.ppermute(x, 'bond', pairs)]
    ppermute x13 -> x12, waiting for transfers between devices: 35.6 us -> 35.4 us  [on_line(): send = lambda x, pairs: lax.ppermute(x, 'bond', pairs)]
  transfers between devices with their start and end apart: 13 -> 12, of which waited for: 4 -> 3; matrix products, arithmetic and copies ran while one was open for 1% -> 1% of each run, Pallas kernels for 20% -> 14%
where the time goes in v2:
time: 98.1 us; the launch traced here: 97.7 us
  Pallas kernels  41.1 us (42%)
  waiting for transfers between devices  35.4 us (36%)
  starting transfers between devices  18.9 us (19%)
  local copies, waits for them, and re-layouts  1.24 us (1%)
  between operations  1.04 us (1%)
    ppermute x12, waiting for transfers between devices, on_line(): send = lambda x, pairs: lax.ppermute(x, 'bond', pairs)  35.4 us
    ppermute x12, starting transfers between devices, on_line(): send = lambda x, pairs: lax.ppermute(x, 'bond', pairs)  18.9 us
    pallas_call x2, Pallas kernels, level(): pl.pallas_call(functools.partial(level_kernel, len(pieces), section > 0,...  14.4 us
    pallas_call x1, Pallas kernels, last_level(): pl.pallas_call(functools.partial(last_kernel, len(pieces), section, rows,...  13.3 us
    pallas_call x2, Pallas kernels, more(): pl.pallas_call(functools.partial(more_kernel, wired, rows, width), out_sh...  12.6 us
  transfers between devices with their start and end apart: 12, of which 3 were waited for; matrix products, arithmetic and copies ran while one was open for 1% of the time, Pallas kernels for 14%

profile of v2, /device:TPU:0, one launch (start us, length us, event | category | flops | bytes accessed | tf_op | source)
XLA Modules:
  0.0 97.7 jit_solution(919850218922678499)
XLA Ops:
  0.6 0.0 copy-start
  0.6 5.1 %collective-permute-start = (f32[16,4096]{1,0:T(8,128)}, f32[16,4096]{1,0:T(8,128)S(1)}, u32[]{:S(2)}, u32[]{:S(2)}) collective-permute-start(f32[16,4096]{1,0:T(8,128)} %refs_0_.1), channel_id=1, source_target_pairs={{0,1},{3,2},{4,5},{7,6},{8,9},{11,10},{12,13},{15,14},{16,17},{19,... | collective-permute-start | bytes 786440 | tf_op jit(solution)/shard_map/ppermute | solution.py:278
  5.8 0.7 collective-permute-start.1
  6.4 4.0 %collective-permute-start.2 = (f32[16,4096]{1,0:T(8,128)}, f32[16,4096]{1,0:T(8,128)S(1)}, u32[]{:S(2)}, u32[]{:S(2)}) collective-permute-start(f32[16,4096]{1,0:T(8,128)} %refs_0_.1), channel_id=1, source_target_pairs={{0,2},{3,1},{4,6},{7,5},{8,10},{11,9},{12,14},{15,13},{16,18},{19,... | collective-permute-start | bytes 786440 | tf_op jit(solution)/shard_map/ppermute | solution.py:278
  10.4 1.2 %slice_bitcast_fusion.2 = (f32[16,4096]{1,0:T(8,128)S(1)}, f32[16,4096]{1,0:T(8,128)S(1)}, f32[16,4096]{1,0:T(8,128)S(1)}) fusion(f32[3,16,4096]{2,1,0:T(8,128)} %param.3), kind=kLoop, calls=%fused_computation.2 | loop fusion | bytes 1572864 | tf_op jit(solution)/shard_map/squeeze | solution.py:297
  11.6 1.4 %collective-permute-start.3 = (f32[16,4096]{1,0:T(8,128)S(1)}, f32[16,4096]{1,0:T(8,128)S(1)}, u32[]{:S(2)}, u32[]{:S(2)}) collective-permute-start(f32[16,4096]{1,0:T(8,128)S(1)} %get-tuple-element.38.refs_4_), channel_id=1, source_target_pairs={{0,1},{3,2},{4,5},{7,6},{8,9},{11,10},{12,13},{15,14},{16,17},{19,... | collective-permute-start | bytes 786440 | tf_op jit(solution)/shard_map/ppermute | solution.py:278
  13.1 1.3 %collective-permute-start.6 = (f32[2,16,4096]{2,1,0:T(8,128)S(1)}, f32[2,16,4096]{2,1,0:T(8,128)S(1)}, u32[]{:S(2)}, u32[]{:S(2)}) collective-permute-start(f32[2,16,4096]{2,1,0:T(8,128)S(1)} %slice.21), channel_id=1, source_target_pairs={{0,1},{3,2},{4,5},{7,6},{8,9},{11,10},{12,13},{15,14},{16,17},{19,... | collective-permute-start | bytes 1572872 | tf_op jit(solution)/shard_map/ppermute | solution.py:278
  14.4 0.0 collective-permute-done.refs_1_
  14.4 0.0 collective-permute-done.1.refs_2_
  14.4 4.0 %collective-permute-done.2.refs_3_ = f32[16,4096]{1,0:T(8,128)S(1)} collective-permute-done((f32[16,4096]{1,0:T(8,128)}, f32[16,4096]{1,0:T(8,128)S(1)}, u32[]{:S(2)}, u32[]{:S(2)}) %collective-permute-start.2) | collective-permute-done | bytes 262176 | tf_op jit(solution)/shard_map/ppermute | solution.py:278
  18.4 7.1 %level.2 = (f32[16,4224]{1,0:T(8,128)S(1)}, f32[8,128]{1,0:T(8,128)S(1)}, bf16[192,4096]{1,0:T(8,128)(2,1)S(1)}, bf16[128,4096]{1,0:T(8,128)(2,1)S(1)}) custom-call(f32[16,4096]{1,0:T(8,128)S(1)} %copy-done, f32[16,4096]{1,0:T(8,128)S(1)} %collective-permute-done.refs_1_, f32[16,4096]{1,0:T(8,128)S(1)} %collective-permute-done.1.refs_2_, ...), custom_call_target="tpu_custom_call" | custom-call | flops 3221225472 | bytes 4194304 | tf_op jit(solution)/shard_map/level/pallas_call | solution.py:206
  25.5 0.0 collective-permute-done.3.u_ref
  25.6 6.3 %more.2 = (f32[16,4224]{1,0:T(8,128)S(1)}, f32[8,128]{1,0:T(8,128)S(1)}) custom-call(bf16[192,4096]{1,0:T(8,128)(2,1)S(1)} %get-tuple-element.20.stacked, bf16[128,4096]{1,0:T(8,128)(2,1)S(1)} %get-tuple-element.21.factor, f32[16,4096]{1,0:T(8,128)S(1)} %collective-permute-done.3.u_ref, f32[8,128]{1,0:T(8,128)S(1)} %get-tuple-element.22.before_ref), custom_call_target="tpu_custom_call" | custom-call | flops 3221225472 | bytes 4194304 | tf_op jit(solution)/shard_map/more/pallas_call | solution.py:256
  31.9 0.7 collective-permute-start.5
  32.6 0.9 collective-permute-start.4
  33.4 0.6 collective-permute-done.6
  34.1 0.0 collective-permute-done.5.refs_3_
  34.1 0.0 collective-permute-done.4.refs_2_
  34.1 7.2 %level.3 = (f32[16,4224]{1,0:T(8,128)S(1)}, f32[8,128]{1,0:T(8,128)S(1)}, bf16[192,4096]{1,0:T(8,128)(2,1)S(1)}, bf16[128,4096]{1,0:T(8,128)(2,1)S(1)}) custom-call(f32[16,4224]{1,0:T(8,128)S(1)} %get-tuple-element.19.refs_0_, f32[16,4224]{1,0:T(8,128)S(1)} %get-tuple-element.23.refs_1_, f32[16,4224]{1,0:T(8,128)S(1)} %collective-permute-done.4.refs_2_, ...), custom_call_target="tpu_custom_call" | custom-call | flops 3221225472 | bytes 4194304 | tf_op jit(solution)/shard_map/level/pallas_call | solution.py:206
  41.3 6.3 %more.3 = (f32[16,4224]{1,0:T(8,128)S(1)}, f32[8,128]{1,0:T(8,128)S(1)}) custom-call(bf16[192,4096]{1,0:T(8,128)(2,1)S(1)} %get-tuple-element.26.stacked, bf16[128,4096]{1,0:T(8,128)(2,1)S(1)} %get-tuple-element.27.factor, f32[16,4096]{1,0:T(8,128)S(1)} %get-tuple-element.40.u_ref, f32[8,128]{1,0:T(8,128)S(1)} %get-tuple-element.28.before_ref), custom_call_target="tpu_custom_call" | custom-call | flops 3221225472 | bytes 4194304 | tf_op jit(solution)/shard_map/more/pallas_call | solution.py:256
  47.6 0.7 collective-permute-start.8
  48.3 0.9 collective-permute-start.7
  49.2 0.0 collective-permute-done.8.refs_3_
  49.2 0.0 collective-permute-done.7.refs_2_
  49.2 13.3 %last.1 = (f32[16,4224]{1,0:T(8,128)S(1)}, f32[16,4096]{1,0:T(8,128)S(1)}, f32[8,128]{1,0:T(8,128)S(1)}) custom-call(f32[16,4224]{1,0:T(8,128)S(1)} %get-tuple-element.25.refs_0_, f32[16,4224]{1,0:T(8,128)S(1)} %get-tuple-element.29.refs_1_, f32[16,4224]{1,0:T(8,128)S(1)} %collective-permute-done.7.refs_2_, f32[16,4224]{1,0:T(8,128)S(1)} %collective-permute-done.8.refs_3_, ...), custom_call_target="tpu_custom_call" | custom-call | flops 6442450944 | bytes 4194304 | tf_op jit(solution)/shard_map/last/pallas_call | solution.py:231
  62.6 1.3 %collective-permute-start.9 = (f32[16,4224]{1,0:T(8,128)S(1)}, f32[16,4224]{1,0:T(8,128)S(1)}, u32[]{:S(2)}, u32[]{:S(2)}) collective-permute-start(f32[16,4224]{1,0:T(8,128)S(1)} %get-tuple-element.32), channel_id=1, source_target_pairs={{1,0},{2,3},{5,4},{6,7},{9,8},{10,11},{13,12},{14,15},{17,16},{18,... | collective-permute-start | bytes 811016 | tf_op jit(solution)/shard_map/ppermute | solution.py:278
  63.9 0.7 collective-permute-start.10
  64.5 1.3 %collective-permute-start.11 = (f32[8,128]{1,0:T(8,128)S(1)}, f32[8,128]{1,0:T(8,128)S(1)}, u32[]{:S(2)}, u32[]{:S(2)}) collective-permute-start(f32[8,128]{1,0:T(8,128)S(1)} %get-tuple-element.33.notes), channel_id=1, source_target_pairs={{1,3},{2,0},{5,7},{6,4},{9,11},{10,8},{13,15},{14,12},{17,19},{18,... | collective-permute-start | bytes 12296 | tf_op jit(solution)/shard_map/ppermute | solution.py:278
  65.8 0.0 collective-permute-done.10.swapped
  65.8 30.8 %collective-permute-done.11.across = f32[8,128]{1,0:T(8,128)S(1)} collective-permute-done((f32[8,128]{1,0:T(8,128)S(1)}, f32[8,128]{1,0:T(8,128)S(1)}, u32[]{:S(2)}, u32[]{:S(2)}) %collective-permute-start.11) | collective-permute-done | bytes 4128 | tf_op jit(solution)/shard_map/ppermute | solution.py:278
  96.6 0.0 collective-permute-done.9.moved_ref
  96.6 0.9 finish.1
  (6 shorter events, 0.1 us)
Async XLA Ops:
  0.6 17.8 %copy-start = (f32[16,4096]{1,0:T(8,128)S(1)}, f32[16,4096]{1,0:T(8,128)}, u32[]{:S(2)}) copy-start(f32[16,4096]{1,0:T(8,128)} %refs_0_.1) | copy-start | bytes 786436
  0.6 12.4 %copy-start.1 = (f32[3,16,4096]{2,1,0:T(8,128)S(1)}, f32[3,16,4096]{2,1,0:T(8,128)}, u32[]{:S(2)}) copy-start(f32[3,16,4096]{2,1,0:T(8,128)} %param.3) | copy-start | bytes 2359300
  0.6 13.8 %collective-permute-start = (f32[16,4096]{1,0:T(8,128)}, f32[16,4096]{1,0:T(8,128)S(1)}, u32[]{:S(2)}, u32[]{:S(2)}) collective-permute-start(f32[16,4096]{1,0:T(8,128)} %refs_0_.1), channel_id=1, source_target_pairs={{0,1},{3,2},{4,5},{7,6},{8,9},{11,10},{12,13},{15,14},{16,17},{19,... | collective-permute-start | bytes 786440 | tf_op jit(solution)/shard_map/ppermute | solution.py:278
  5.8 8.7 %collective-permute-start.1 = (f32[16,4096]{1,0:T(8,128)}, f32[16,4096]{1,0:T(8,128)S(1)}, u32[]{:S(2)}, u32[]{:S(2)}) collective-permute-start(f32[16,4096]{1,0:T(8,128)} %refs_0_.1), channel_id=1, source_target_pairs={{1,2},{2,1},{5,6},{6,5},{9,10},{10,9},{13,14},{14,13},{17,18},{18,... | collective-permute-start | bytes 786440 | tf_op jit(solution)/shard_map/ppermute | solution.py:278
  6.4 12.0 %collective-permute-start.2 = (f32[16,4096]{1,0:T(8,128)}, f32[16,4096]{1,0:T(8,128)S(1)}, u32[]{:S(2)}, u32[]{:S(2)}) collective-permute-start(f32[16,4096]{1,0:T(8,128)} %refs_0_.1), channel_id=1, source_target_pairs={{0,2},{3,1},{4,6},{7,5},{8,10},{11,9},{12,14},{15,13},{16,18},{19,... | collective-permute-start | bytes 786440 | tf_op jit(solution)/shard_map/ppermute | solution.py:278
  11.6 13.9 %collective-permute-start.3 = (f32[16,4096]{1,0:T(8,128)S(1)}, f32[16,4096]{1,0:T(8,128)S(1)}, u32[]{:S(2)}, u32[]{:S(2)}) collective-permute-start(f32[16,4096]{1,0:T(8,128)S(1)} %get-tuple-element.38.refs_4_), channel_id=1, source_target_pairs={{0,1},{3,2},{4,5},{7,6},{8,9},{11,10},{12,13},{15,14},{16,17},{19,... | collective-permute-start | bytes 786440 | tf_op jit(solution)/shard_map/ppermute | solution.py:278
  13.1 20.9 %collective-permute-start.6 = (f32[2,16,4096]{2,1,0:T(8,128)S(1)}, f32[2,16,4096]{2,1,0:T(8,128)S(1)}, u32[]{:S(2)}, u32[]{:S(2)}) collective-permute-start(f32[2,16,4096]{2,1,0:T(8,128)S(1)} %slice.21), channel_id=1, source_target_pairs={{0,1},{3,2},{4,5},{7,6},{8,9},{11,10},{12,13},{15,14},{16,17},{19,... | collective-permute-start | bytes 1572872 | tf_op jit(solution)/shard_map/ppermute | solution.py:278
  31.9 2.2 %collective-permute-start.5 = (f32[16,4224]{1,0:T(8,128)S(1)}, f32[16,4224]{1,0:T(8,128)S(1)}, u32[]{:S(2)}, u32[]{:S(2)}) collective-permute-start(f32[16,4224]{1,0:T(8,128)S(1)} %get-tuple-element.23.refs_1_), channel_id=1, source_target_pairs={{1,2},{2,1},{5,6},{6,5},{9,10},{10,9},{13,14},{14,13},{17,18},{18,... | collective-permute-start | bytes 811016 | tf_op jit(solution)/shard_map/ppermute | solution.py:278
  32.6 1.5 %collective-permute-start.4 = (f32[16,4224]{1,0:T(8,128)S(1)}, f32[16,4224]{1,0:T(8,128)S(1)}, u32[]{:S(2)}, u32[]{:S(2)}) collective-permute-start(f32[16,4224]{1,0:T(8,128)S(1)} %get-tuple-element.19.refs_0_), channel_id=1, source_target_pairs={{1,2},{2,1},{5,6},{6,5},{9,10},{10,9},{13,14},{14,13},{17,18},{18,... | collective-permute-start | bytes 811016 | tf_op jit(solution)/shard_map/ppermute | solution.py:278
  47.6 1.6 %collective-permute-start.8 = (f32[16,4224]{1,0:T(8,128)S(1)}, f32[16,4224]{1,0:T(8,128)S(1)}, u32[]{:S(2)}, u32[]{:S(2)}) collective-permute-start(f32[16,4224]{1,0:T(8,128)S(1)} %get-tuple-element.29.refs_1_), channel_id=1, source_target_pairs={{1,2},{2,1},{5,6},{6,5},{9,10},{10,9},{13,14},{14,13},{17,18},{18,... | collective-permute-start | bytes 811016 | tf_op jit(solution)/shard_map/ppermute | solution.py:278
  48.3 0.9 collective-permute-start.7
  62.6 34.1 %collective-permute-start.9 = (f32[16,4224]{1,0:T(8,128)S(1)}, f32[16,4224]{1,0:T(8,128)S(1)}, u32[]{:S(2)}, u32[]{:S(2)}) collective-permute-start(f32[16,4224]{1,0:T(8,128)S(1)} %get-tuple-element.32), channel_id=1, source_target_pairs={{1,0},{2,3},{5,4},{6,7},{9,8},{10,11},{13,12},{14,15},{17,16},{18,... | collective-permute-start | bytes 811016 | tf_op jit(solution)/shard_map/ppermute | solution.py:278
  63.9 2.0 %collective-permute-start.10 = (f32[8,128]{1,0:T(8,128)S(1)}, f32[8,128]{1,0:T(8,128)S(1)}, u32[]{:S(2)}, u32[]{:S(2)}) collective-permute-start(f32[8,128]{1,0:T(8,128)S(1)} %get-tuple-element.33.notes), channel_id=1, source_target_pairs={{1,2},{2,1},{5,6},{6,5},{9,10},{10,9},{13,14},{14,13},{17,18},{18,... | collective-permute-start | bytes 12296 | tf_op jit(solution)/shard_map/ppermute | solution.py:278
  64.5 32.1 %collective-permute-start.11 = (f32[8,128]{1,0:T(8,128)S(1)}, f32[8,128]{1,0:T(8,128)S(1)}, u32[]{:S(2)}, u32[]{:S(2)}) collective-permute-start(f32[8,128]{1,0:T(8,128)S(1)} %get-tuple-element.33.notes), channel_id=1, source_target_pairs={{1,3},{2,0},{5,7},{6,4},{9,11},{10,8},{13,15},{14,12},{17,19},{18,... | collective-permute-start | bytes 12296 | tf_op jit(solution)/shard_map/ppermute | solution.py:278
